TPU v7x, 32 devices: a whole 2x2x4 slice. The times are simulated.
32 devices in a mesh: grp: 8 (over y, x, core), mem: 4 (over z).
Axes of the slice: x: 2, y: 2, z: 4, core: 2. Of those that a mesh axis runs over, the one named last changes fastest.
Arguments:
- residual: float32 [256, 64, 256], P(('grp', 'mem')), may hold values from -6 to 6
- direction: float32 [256, 64, 256], P(('grp', 'mem')), may hold values from -6 to 6
- local_inverse: bfloat16 [256, 256, 256], P(('grp', 'mem')), may hold values from -1 to 16, as said below
- dirichlet: bfloat16 [256, 256, 256], P(('grp', 'mem')), may hold values from -1 to 16, as said below
- coupling: bfloat16 [256, 24, 256], P(('grp', 'mem')), may hold values from -0.375 to 0.375
- corner_map: int32 [256, 24], P(('grp', 'mem')), may hold values from 0 to 6143
- coarse_factor: bfloat16 [8, 2048, 2048], P('grp'), may hold values from -1 to 3, as said below
Outputs:
- new_residual: float32 [256, 64, 256], P(('grp', 'mem'))
- new_direction: float32 [256, 64, 256], P(('grp', 'mem'))
- step_sizes: float32 [3, 64], replicated
Inputs may be any that keep to these rules, and one draw needn't show every extreme that they name: `local_inverse`: each subdomain's matrix is symmetric positive definite. `dirichlet`: each subdomain's matrix is symmetric positive definite. `coarse_factor`: each group's factor is lower triangular with a positive diagonal.
All inputs are finite; a program needn't handle non-finite values.
Results may differ from a plain program's by a relative error of at most 0.0083.
Values sent between devices are 32-bit elements; how exact they have to be, the bound alone decides.
A program may use at most 128 MiB of HBM per device.

v0:
```python
import jax
import jax.numpy as jnp
from jax import lax
from jax.sharding import PartitionSpec as P

ITERS = 3
highest = lax.Precision.HIGHEST


def from_behind(block, axis, distance):
    devices = range(lax.axis_size(axis))
    route = [((i - distance) % len(devices), i) for i in devices]
    return lax.ppermute(block, axis, route)


def extended(cells, sides, width):
    for axis, dim in sides:
        count = lax.axis_size(axis)
        head = lax.slice_in_dim(cells, 0, width, axis=dim)
        tail = lax.slice_in_dim(cells, cells.shape[dim] - width, cells.shape[dim], axis=dim)
        cells = jnp.concatenate(
            [
                lax.ppermute(tail, axis, [(i, (i + 1) % count) for i in range(count)]),
                cells,
                lax.ppermute(head, axis, [((i + 1) % count, i) for i in range(count)]),
            ],
            axis=dim,
        )
    return cells


def solve_local(matrices, vectors):
    return jnp.einsum(
        "sij,skj->ski", matrices, vectors.astype(jnp.bfloat16), preferred_element_type=jnp.float32
    )


def column_sums(left_side, right_side):
    return jnp.sum(left_side * right_side, axis=(0, 2))


def coarse_solve(factor, coarse_load):
    forward = jax.scipy.linalg.solve_triangular(factor, coarse_load.T, lower=True)
    return jax.scipy.linalg.solve_triangular(factor, forward, lower=True, trans=1).T


def fold_neighbours(partial_value, block_size):
    from_upper = from_behind(partial_value[:, :block_size], "grp", -1)
    from_lower = from_behind(partial_value[:, 2 * block_size :], "grp", 1)
    return partial_value[:, block_size : 2 * block_size] + from_upper + from_lower


def local(residual, direction, local_inverse, dirichlet, coupling, corner_map, coarse_factor):
    sub_count, rhs_count, dofs_count = residual.shape
    corner_count = coupling.shape[1]
    block_size = coarse_factor.shape[1]
    factor = coarse_factor[0].astype(jnp.float32)
    flat_map = corner_map.reshape(-1)
    coupling_wide = coupling.astype(jnp.float32)
    precond = solve_local(dirichlet, residual)
    norm_now = lax.psum(column_sums(residual, precond), ("grp", "mem"))
    step_list = []
    for iteration in range(ITERS):
        solved = solve_local(local_inverse, direction)
        partial_corner = jnp.einsum("ski,sci->skc", solved, coupling_wide, precision=highest)
        flat_corner = partial_corner.transpose(1, 0, 2).reshape(rhs_count, sub_count * corner_count)
        partial_value = (
            jnp.zeros((rhs_count, 3 * block_size), jnp.float32).at[:, flat_map].add(flat_corner)
        )
        folded = fold_neighbours(partial_value, block_size)
        solution = coarse_solve(factor, lax.psum(folded, "mem"))
        widened = extended(solution, (("grp", 1),), block_size)
        picked = widened[:, flat_map].reshape(rhs_count, sub_count, corner_count).transpose(1, 0, 2)
        lifted = jnp.einsum("skc,sci->ski", picked, coupling_wide, precision=highest)
        image = solve_local(local_inverse, direction + lifted)
        curvature = lax.psum(column_sums(direction, image), ("grp", "mem"))
        alpha = norm_now / curvature
        step_list.append(alpha)
        residual = residual - alpha[None, :, None] * image
        precond = solve_local(dirichlet, residual)
        norm_next = lax.psum(column_sums(residual, precond), ("grp", "mem"))
        direction = precond + (norm_next / norm_now)[None, :, None] * direction
        norm_now = norm_next
    return (residual, direction, jnp.stack(step_list))


def solution(mesh):
    return jax.shard_map(
        local,
        mesh=mesh,
        in_specs=(
            P(("grp", "mem"), None, None),
            P(("grp", "mem"), None, None),
            P(("grp", "mem"), None, None),
            P(("grp", "mem"), None, None),
            P(("grp", "mem"), None, None),
            P(("grp", "mem"), None),
            P("grp", None, None),
        ),
        out_specs=(P(("grp", "mem"), None, None), P(("grp", "mem"), None, None), P()),
        check_vma=False,
    )
```

profile of v0, /device:TPU:0, one launch (start us, length us, event | category | flops | bytes accessed | tf_op | source)
XLA Modules:
  0.0 917.9 jit_solution(7679273841835778049)
XLA Ops:
  11.1 3.0 scatter_custom_fusion
  14.1 3.0 fusion.365
  21.1 2.9 collective-permute-start
  24.0 11.3 %convert_select_fusion = f32[2048,2048]{1,0:T(8,128)} fusion(bf16[1,2048,2048]{2,1,0:T(8,128)(2,1)} %param.17), kind=kLoop, calls=%fused_computation.8 | loop fusion | flops 12582912 | bytes 25165824 | tf_op jit(solution)/shard_map/jit(_solve_triangular)/triangular_solve | solution.py:44
  37.6 55.7 %while.12 = (s32[]{:T(128)}, f32[2048,2048]{1,0:T(8,128)}, s32[16,2]{0,1:T(2,128)S(1)}, f32[16,128,128]{2,1,0:T(8,128)}, s32[]{:T(128)}) while((s32[]{:T(128)}, f32[2048,2048]{1,0:T(8,128)}, s32[16,2]{0,1:T(2,128)S(1)}, f32[16,128,128]{2,1,0:T(8,128)}, s32[]{:T(128)}) %tuple.417), condition=%wide.while_cond.1, body=%wide.while_body.1.sunk | while | flops 2 | bytes 132205 | solution.py:44
  38.2 2.9 bitcast_dynamic-update-slice_fusion.2
  41.7 2.9 bitcast_dynamic-update-slice_fusion.2
  45.2 2.9 bitcast_dynamic-update-slice_fusion.2
  48.7 2.9 bitcast_dynamic-update-slice_fusion.2
  52.2 2.9 bitcast_dynamic-update-slice_fusion.2
  55.7 2.9 bitcast_dynamic-update-slice_fusion.2
  59.2 2.9 bitcast_dynamic-update-slice_fusion.2
  62.6 2.9 bitcast_dynamic-update-slice_fusion.2
  66.1 2.9 bitcast_dynamic-update-slice_fusion.2
  69.6 2.9 bitcast_dynamic-update-slice_fusion.2
  73.1 2.9 bitcast_dynamic-update-slice_fusion.2
  76.6 2.9 bitcast_dynamic-update-slice_fusion.2
  80.1 2.9 bitcast_dynamic-update-slice_fusion.2
  83.6 2.9 bitcast_dynamic-update-slice_fusion.2
  87.0 2.9 bitcast_dynamic-update-slice_fusion.2
  90.5 2.8 bitcast_dynamic-update-slice_fusion.2
  93.3 158.4 %custom-call.11 = f32[16,128,128]{1,2,0:T(8,128)S(1)} custom-call(f32[16,128,128]{2,1,0:T(8,128)} %get-tuple-element.46), custom_call_target="InvertDiagBlocksLowerTriangular" | custom-call | tf_op jit(solution)/shard_map/jit(_solve_triangular)/triangular_solve | solution.py:44
  308.3 11.7 %collective-permute-done.3 = f32[64,2048]{1,0:T(8,128)S(1)} collective-permute-done((f32[64,2048]{1,0:T(8,128)S(1)}, f32[64,2048]{1,0:T(8,128)S(1)}, u32[]{:S(2)}, u32[]{:S(2)}) %collective-permute-start.3) | collective-permute-done | bytes 524320 | tf_op jit(solution)/shard_map/ppermute | solution.py:25
  322.5 3.2 copy.31
  325.7 2.6 gather_fusion
  332.1 39.5 %all-reduce = (f32[64]{0:T(128)S(1)}, f32[64]{0:T(128)S(1)}) all-reduce(f32[64]{0:T(128)S(1)} %fusion.9, f32[64]{0:T(128)S(1)} %get-tuple-element.437), channel_id=1, replica_groups=mesh['grp'=8,'mem'=4] {'grp','mem'}, use_global_device_ids=true, to_apply=%region_1.0 | all-reduce | flops 128 | bytes 1024 | tf_op jit(solution)/shard_map/psum | solution.py:61
  375.1 40.9 %psum.73 = f32[64]{0:T(128)S(1)} all-reduce(f32[64]{0:T(128)S(1)} %get-tuple-element.439), channel_id=1, replica_groups=mesh['grp'=8,'mem'=4] {'grp','mem'}, use_global_device_ids=true, to_apply=%region_7.0 | all-reduce | flops 64 | bytes 512 | tf_op jit(solution)/shard_map/psum | solution.py:81
  419.0 3.0 scatter_custom_fusion.1
  422.0 3.6 fusion.364
  430.3 2.6 collective-permute-start.4
  435.3 8.7 collective-permute-done.5
  447.3 38.6 %all-reduce.7.cloned.1.call-done = f32[2048,64]{0,1:T(8,128)} async-done(((f32[2048,64]{0,1:T(8,128)}), f32[2048,64]{0,1:T(8,128)}) %all-reduce.7.cloned.1.call-update) | async-done | bytes 524304 | tf_op jit(solution)/shard_map/psum | solution.py:71
  556.5 12.2 %collective-permute-done.7 = f32[64,2048]{1,0:T(8,128)S(1)} collective-permute-done((f32[64,2048]{1,0:T(8,128)S(1)}, f32[64,2048]{1,0:T(8,128)S(1)}, u32[]{:S(2)}, u32[]{:S(2)}) %collective-permute-start.7) | collective-permute-done | bytes 524320 | tf_op jit(solution)/shard_map/ppermute | solution.py:25
  572.0 3.2 copy.35
  575.3 2.6 gather_fusion.1
  579.3 2.4 multiply_reduce_fusion.3
  581.7 39.3 %psum.75 = f32[64]{0:T(128)S(1)} all-reduce(f32[64]{0:T(128)S(1)} %get-tuple-element.479), channel_id=1, replica_groups=mesh['grp'=8,'mem'=4] {'grp','mem'}, use_global_device_ids=true, to_apply=%region_11.0 | all-reduce | flops 64 | bytes 512 | tf_op jit(solution)/shard_map/psum | solution.py:76
  624.5 38.9 %psum.76 = f32[64]{0:T(128)S(1)} all-reduce(f32[64]{0:T(128)S(1)} %get-tuple-element.481), channel_id=1, replica_groups=mesh['grp'=8,'mem'=4] {'grp','mem'}, use_global_device_ids=true, to_apply=%region_13.0 | all-reduce | flops 64 | bytes 512 | tf_op jit(solution)/shard_map/psum | solution.py:81
  666.4 3.0 scatter_custom_fusion.2
  669.4 3.6 fusion.363
  677.7 2.8 collective-permute-start.8
  682.9 7.5 collective-permute-done.9
  694.3 39.1 %all-reduce.9.cloned.1.call-done = f32[2048,64]{0,1:T(8,128)} async-done(((f32[2048,64]{0,1:T(8,128)}), f32[2048,64]{0,1:T(8,128)}) %all-reduce.9.cloned.1.call-update) | async-done | bytes 524304 | tf_op jit(solution)/shard_map/psum | solution.py:71
  804.0 12.3 %collective-permute-done.11 = f32[64,2048]{1,0:T(8,128)S(1)} collective-permute-done((f32[64,2048]{1,0:T(8,128)S(1)}, f32[64,2048]{1,0:T(8,128)S(1)}, u32[]{:S(2)}, u32[]{:S(2)}) %collective-permute-start.11) | collective-permute-done | bytes 524320 | tf_op jit(solution)/shard_map/ppermute | solution.py:25
  819.5 3.2 copy.39
  822.8 2.6 gather_fusion.2
  828.4 39.3 %psum.78 = f32[64]{0:T(128)S(1)} all-reduce(f32[64]{0:T(128)S(1)} %get-tuple-element.521), channel_id=1, replica_groups=mesh['grp'=8,'mem'=4] {'grp','mem'}, use_global_device_ids=true, to_apply=%region_17.0 | all-reduce | flops 64 | bytes 512 | tf_op jit(solution)/shard_map/psum | solution.py:76
  869.4 38.9 %psum.79 = f32[64]{0:T(128)S(1)} all-reduce(f32[64]{0:T(128)S(1)} %get-tuple-element.523), channel_id=1, replica_groups=mesh['grp'=8,'mem'=4] {'grp','mem'}, use_global_device_ids=true, to_apply=%region_19.0 | all-reduce | flops 64 | bytes 512 | tf_op jit(solution)/shard_map/psum | solution.py:81
  (652 shorter events, 269.4 us)
Async XLA Ops:
  7.2 1.2 copy-start
  7.2 244.6 %all-reduce.5.cloned.1.call-start = ((), (), s32[]{:S(2)}) async-start(), calls=%async_computation | async-start | bytes 1048576 | tf_op jit(solution)/shard_map/psum | solution.py:71
  19.5 16.1 %collective-permute-start.1 = (f32[64,2048]{1,0:T(8,128)}, f32[64,2048]{1,0:T(8,128)}, u32[]{:S(2)}, u32[]{:S(2)}) collective-permute-start(f32[64,2048]{1,0:T(8,128)} %copy.30), channel_id=1, source_target_pairs={{28,0},{0,4},{4,8},{8,12},{12,16},{16,20},{20,24},{24,28},{29,1},{... | collective-permute-start | bytes 1572872 | tf_op jit(solution)/shard_map/ppermute | solution.py:13
  21.1 14.5 %collective-permute-start = (f32[64,2048]{1,0:T(8,128)}, f32[64,2048]{1,0:T(8,128)S(1)}, u32[]{:S(2)}, u32[]{:S(2)}) collective-permute-start(f32[64,2048]{1,0:T(8,128)} %copy.29), channel_id=1, source_target_pairs={{4,0},{8,4},{12,8},{16,12},{20,16},{24,20},{28,24},{0,28},{5,1},{9... | collective-permute-start | bytes 1572872 | tf_op jit(solution)/shard_map/ppermute | solution.py:13
  37.6 448.3 %all-reduce.7.cloned.1.call-start = ((), (), s32[]{:S(2)}) async-start(), calls=%async_computation.1 | async-start | bytes 1048576 | tf_op jit(solution)/shard_map/psum | solution.py:71
  251.8 39.4 %copy-start.1 = (f32[2048,2048]{1,0:T(8,128)S(1)}, f32[2048,2048]{1,0:T(8,128)}, u32[]{:S(2)}) copy-start(f32[2048,2048]{1,0:T(8,128)} %get-tuple-element.572) | copy-start | bytes 50331652
  272.1 35.6 %copy-start.2 = (bf16[8,256,256]{2,1,0:T(8,128)(2,1)S(1)}, bf16[8,256,256]{2,1,0:T(8,128)(2,1)}, u32[]{:S(2)}) copy-start(bf16[8,256,256]{2,1,0:T(8,128)(2,1)} %param.14) | copy-start | bytes 3145732
  272.1 35.6 %copy-start.9 = (f32[8,64,256]{2,1,0:T(8,128)S(1)}, f32[8,64,256]{2,1,0:T(8,128)}, u32[]{:S(2)}) copy-start(f32[8,64,256]{2,1,0:T(8,128)} %param.11) | copy-start | bytes 1572868
  292.3 35.9 %copy-start.7 = (bf16[8,24,256]{2,1,0:T(8,128)(2,1)S(1)}, bf16[8,24,256]{2,1,0:T(8,128)(2,1)}, u32[]{:S(2)}) copy-start(bf16[8,24,256]{2,1,0:T(8,128)(2,1)} %param.15) | copy-start | bytes 294916
  306.0 13.9 %collective-permute-start.3 = (f32[64,2048]{1,0:T(8,128)S(1)}, f32[64,2048]{1,0:T(8,128)S(1)}, u32[]{:S(2)}, u32[]{:S(2)}) collective-permute-start(f32[64,2048]{1,0:T(8,128)S(1)} %bitcast.583), channel_id=1, source_target_pairs={{4,0},{8,4},{12,8},{16,12},{20,16},{24,20},{28,24},{0,28},{5,1},{9... | collective-permute-start | bytes 1572872 | tf_op jit(solution)/shard_map/ppermute | solution.py:25
  307.7 13.5 %collective-permute-start.2 = (f32[64,2048]{1,0:T(8,128)S(1)}, f32[64,2048]{1,0:T(8,128)S(1)}, u32[]{:S(2)}, u32[]{:S(2)}) collective-permute-start(f32[64,2048]{1,0:T(8,128)S(1)} %bitcast.584), channel_id=1, source_target_pairs={{0,4},{4,8},{8,12},{12,16},{16,20},{20,24},{24,28},{28,0},{1,5},{5... | collective-permute-start | bytes 1572872 | tf_op jit(solution)/shard_map/ppermute | solution.py:23
  373.0 0.8 copy-start.6
  417.4 0.8 copy-start.4
  430.3 13.7 %collective-permute-start.5 = (f32[64,2048]{1,0:T(8,128)}, f32[64,2048]{1,0:T(8,128)}, u32[]{:S(2)}, u32[]{:S(2)}) collective-permute-start(f32[64,2048]{1,0:T(8,128)} %copy.34), channel_id=1, source_target_pairs={{28,0},{0,4},{4,8},{8,12},{12,16},{16,20},{20,24},{24,28},{29,1},{... | collective-permute-start | bytes 1572872 | tf_op jit(solution)/shard_map/ppermute | solution.py:13
  430.3 14.3 %collective-permute-start.4 = (f32[64,2048]{1,0:T(8,128)}, f32[64,2048]{1,0:T(8,128)}, u32[]{:S(2)}, u32[]{:S(2)}) collective-permute-start(f32[64,2048]{1,0:T(8,128)} %copy.33), channel_id=1, source_target_pairs={{4,0},{8,4},{12,8},{16,12},{20,16},{24,20},{28,24},{0,28},{5,1},{9... | collective-permute-start | bytes 1572872 | tf_op jit(solution)/shard_map/ppermute | solution.py:13
  446.9 286.5 %all-reduce.9.cloned.1.call-start = ((), (), s32[]{:S(2)}) async-start(), calls=%async_computation.2 | async-start | bytes 1048576 | tf_op jit(solution)/shard_map/psum | solution.py:71
  555.6 13.2 %collective-permute-start.7 = (f32[64,2048]{1,0:T(8,128)S(1)}, f32[64,2048]{1,0:T(8,128)S(1)}, u32[]{:S(2)}, u32[]{:S(2)}) collective-permute-start(f32[64,2048]{1,0:T(8,128)S(1)} %bitcast.586), channel_id=1, source_target_pairs={{4,0},{8,4},{12,8},{16,12},{20,16},{24,20},{28,24},{0,28},{5,1},{9... | collective-permute-start | bytes 1572872 | tf_op jit(solution)/shard_map/ppermute | solution.py:25
  556.5 14.3 %collective-permute-start.6 = (f32[64,2048]{1,0:T(8,128)S(1)}, f32[64,2048]{1,0:T(8,128)S(1)}, u32[]{:S(2)}, u32[]{:S(2)}) collective-permute-start(f32[64,2048]{1,0:T(8,128)S(1)} %bitcast.587), channel_id=1, source_target_pairs={{0,4},{4,8},{8,12},{12,16},{16,20},{20,24},{24,28},{28,0},{1,5},{5... | collective-permute-start | bytes 1572872 | tf_op jit(solution)/shard_map/ppermute | solution.py:23
  622.4 0.8 copy-start.5
  664.8 0.8 copy-start.3
  677.7 12.7 %collective-permute-start.9 = (f32[64,2048]{1,0:T(8,128)}, f32[64,2048]{1,0:T(8,128)}, u32[]{:S(2)}, u32[]{:S(2)}) collective-permute-start(f32[64,2048]{1,0:T(8,128)} %copy.38), channel_id=1, source_target_pairs={{28,0},{0,4},{4,8},{8,12},{12,16},{16,20},{20,24},{24,28},{29,1},{... | collective-permute-start | bytes 1572872 | tf_op jit(solution)/shard_map/ppermute | solution.py:13
  677.7 14.3 %collective-permute-start.8 = (f32[64,2048]{1,0:T(8,128)}, f32[64,2048]{1,0:T(8,128)}, u32[]{:S(2)}, u32[]{:S(2)}) collective-permute-start(f32[64,2048]{1,0:T(8,128)} %copy.37), channel_id=1, source_target_pairs={{4,0},{8,4},{12,8},{16,12},{20,16},{24,20},{28,24},{0,28},{5,1},{9... | collective-permute-start | bytes 1572872 | tf_op jit(solution)/shard_map/ppermute | solution.py:13
  803.1 13.2 %collective-permute-start.11 = (f32[64,2048]{1,0:T(8,128)S(1)}, f32[64,2048]{1,0:T(8,128)S(1)}, u32[]{:S(2)}, u32[]{:S(2)}) collective-permute-start(f32[64,2048]{1,0:T(8,128)S(1)} %bitcast.580), channel_id=1, source_target_pairs={{4,0},{8,4},{12,8},{16,12},{20,16},{24,20},{28,24},{0,28},{5,1},{9... | collective-permute-start | bytes 1572872 | tf_op jit(solution)/shard_map/ppermute | solution.py:25
  804.0 14.3 %collective-permute-start.10 = (f32[64,2048]{1,0:T(8,128)S(1)}, f32[64,2048]{1,0:T(8,128)S(1)}, u32[]{:S(2)}, u32[]{:S(2)}) collective-permute-start(f32[64,2048]{1,0:T(8,128)S(1)} %bitcast.581), channel_id=1, source_target_pairs={{0,4},{4,8},{8,12},{12,16},{16,20},{20,24},{24,28},{28,0},{1,5},{5... | collective-permute-start | bytes 1572872 | tf_op jit(solution)/shard_map/ppermute | solution.py:23
  868.9 42.0 %copy-start.8 = (f32[8,64,256]{2,1,0:T(8,128)}, f32[8,64,256]{2,1,0:T(8,128)S(1)}, u32[]{:S(2)}) copy-start(f32[8,64,256]{2,1,0:T(8,128)S(1)} %multiply_subtract_fusion) | copy-start | bytes 1572868
Sparse Core Ops, SparseCore 0:
  37.7 39.7 all-reduce.4
  447.0 38.8 all-reduce.6
  694.4 38.9 all-reduce.8
where the time goes:
time: 931 us; the launch traced here: 918 us
  blocking collectives  237 us (25%)
  matrix products  207 us (22%)
  other arithmetic  198 us (21%)
  waiting for transfers between devices  138 us (15%)
  local copies, waits for them, and re-layouts  107 us (11%)
  between operations  18.2 us (2%)
  starting transfers between devices  12.9 us (1%)
    another operation x4, other arithmetic, coarse_solve(): jax.scipy.linalg.solve_triangular(factor, forward, lower=True, trans=1)  170 us
    another operation x93, matrix products, coarse_solve(): jax.scipy.linalg.solve_triangular(factor, coarse_load.T, lower=True)  124 us
    psum x3, blocking collectives, local(): norm_next = lax.psum(column_sums(residual, precond), ('grp', 'mem'))  119 us
    psum x2, blocking collectives, local(): curvature = lax.psum(column_sums(direction, image), ('grp', 'mem'))  78.5 us
    psum x3, waiting for transfers between devices, local(): solution = coarse_solve(factor, lax.psum(folded, 'mem'))  77.7 us
    another operation x93, matrix products, coarse_solve(): jax.scipy.linalg.solve_triangular(factor, forward, lower=True, trans=1)  64.3 us
    another operation x85, local copies, waits for them, and re-layouts, coarse_solve(): jax.scipy.linalg.solve_triangular(factor, forward, lower=True, trans=1)  55.9 us
    psum x1, blocking collectives, local(): norm_now = lax.psum(column_sums(residual, precond), ('grp', 'mem'))  39.5 us
  transfers between devices with their start and end apart: 15, of which 12 were waited for; matrix products, arithmetic and copies ran while one was open for 25% of the time, Pallas kernels for 0%

commit v1 on v0

--- a/solution.py
+++ b/solution.py
@@ -73,7 +73,7 @@
         picked = widened[:, flat_map].reshape(rhs_count, sub_count, corner_count).transpose(1, 0, 2)
         lifted = jnp.einsum("skc,sci->ski", picked, coupling_wide, precision=highest)
         image = solve_local(local_inverse, direction + lifted)
-        curvature = lax.psum(column_sums(direction, image), ("grp", "mem"))
+        curvature = jnp.sum(lax.all_gather(column_sums(direction, image), ("grp", "mem")), axis=0)
         alpha = norm_now / curvature
         step_list.append(alpha)
         residual = residual - alpha[None, :, None] * image

time: 931 us -> 938 us (level)
  local copies, waits for them, and re-layouts: 107 us -> 118 us
  waiting for transfers between devices: 138 us -> 127 us
    unnamed x0 -> x2, blocking collectives: none -> 80.7 us
    psum x2 -> x0, blocking collectives: 78.5 us -> none  [local(): curvature = lax.psum(column_sums(direction, image), ('grp', 'mem'))]
    ppermute x3, waiting for transfers between devices: 36.2 us -> 0.01 us  [extended(): lax.ppermute(head, axis, [((i + 1) % count, i) for i in range(count)])]
    ppermute x3, waiting for transfers between devices: 5.2 us -> 31.6 us  [extended(): lax.ppermute(tail, axis, [(i, (i + 1) % count) for i in range(count)])]
    unnamed x329 -> x333, local copies, waits for them, and re-layouts: 10.1 us -> 19.5 us
  transfers between devices with their start and end apart: 15 -> 15, of which waited for: 12 -> 10; matrix products, arithmetic and copies ran while one was open for 25% -> 26% of each run, Pallas kernels for 0% -> 0%
where the time goes in v1:
time: 938 us; the launch traced here: 925 us
  blocking collectives  240 us (26%)
  matrix products  209 us (22%)
  other arithmetic  199 us (21%)
  waiting for transfers between devices  127 us (14%)
  local copies, waits for them, and re-layouts  118 us (13%)
  between operations  17.9 us (2%)
  starting transfers between devices  13.7 us (1%)
    another operation x4, other arithmetic, coarse_solve(): jax.scipy.linalg.solve_triangular(factor, forward, lower=True, trans=1)  169 us
    another operation x93, matrix products, coarse_solve(): jax.scipy.linalg.solve_triangular(factor, coarse_load.T, lower=True)  124 us
    psum x3, blocking collectives, local(): norm_next = lax.psum(column_sums(residual, precond), ('grp', 'mem'))  120 us
    unnamed x2, blocking collectives  80.7 us
    psum x3, waiting for transfers between devices, local(): solution = coarse_solve(factor, lax.psum(folded, 'mem'))  74 us
    another operation x93, matrix products, coarse_solve(): jax.scipy.linalg.solve_triangular(factor, forward, lower=True, trans=1)  65.3 us
    another operation x85, local copies, waits for them, and re-layouts, coarse_solve(): jax.scipy.linalg.solve_triangular(factor, forward, lower=True, trans=1)  57.2 us
    psum x1, blocking collectives, local(): norm_now = lax.psum(column_sums(residual, precond), ('grp', 'mem'))  39.6 us
  transfers between devices with their start and end apart: 15, of which 10 were waited for; matrix products, arithmetic and copies ran while one was open for 26% of the time, Pallas kernels for 0%

profile of v1, /device:TPU:0, one launch (start us, length us, event | category | flops | bytes accessed | tf_op | source)
XLA Modules:
  0.0 924.7 jit_solution(10026663433563119367)
XLA Ops:
  11.1 3.0 scatter_custom_fusion
  14.2 3.0 fusion.365
  19.5 3.4 collective-permute-start
  24.0 11.3 %convert_select_fusion = f32[2048,2048]{1,0:T(8,128)} fusion(bf16[1,2048,2048]{2,1,0:T(8,128)(2,1)} %param.17), kind=kLoop, calls=%fused_computation.8 | loop fusion | flops 12582912 | bytes 25165824 | tf_op jit(solution)/shard_map/jit(_solve_triangular)/triangular_solve | solution.py:44
  38.4 56.4 %while.12 = (s32[]{:T(128)}, f32[2048,2048]{1,0:T(8,128)}, s32[16,2]{0,1:T(2,128)S(1)}, f32[16,128,128]{2,1,0:T(8,128)}, s32[]{:T(128)}) while((s32[]{:T(128)}, f32[2048,2048]{1,0:T(8,128)}, s32[16,2]{0,1:T(2,128)S(1)}, f32[16,128,128]{2,1,0:T(8,128)}, s32[]{:T(128)}) %tuple.417), condition=%wide.while_cond.1, body=%wide.while_body.1.sunk | while | flops 2 | bytes 132705 | solution.py:44
  39.1 2.9 bitcast_dynamic-update-slice_fusion.2
  42.6 2.9 bitcast_dynamic-update-slice_fusion.2
  46.1 2.9 bitcast_dynamic-update-slice_fusion.2
  49.7 2.9 bitcast_dynamic-update-slice_fusion.2
  53.2 2.9 bitcast_dynamic-update-slice_fusion.2
  56.7 2.9 bitcast_dynamic-update-slice_fusion.2
  60.3 2.9 bitcast_dynamic-update-slice_fusion.2
  63.8 2.9 bitcast_dynamic-update-slice_fusion.2
  67.3 2.9 bitcast_dynamic-update-slice_fusion.2
  70.8 2.9 bitcast_dynamic-update-slice_fusion.2
  74.4 2.9 bitcast_dynamic-update-slice_fusion.2
  77.9 2.9 bitcast_dynamic-update-slice_fusion.2
  81.4 2.9 bitcast_dynamic-update-slice_fusion.2
  84.9 2.9 bitcast_dynamic-update-slice_fusion.2
  88.5 2.9 bitcast_dynamic-update-slice_fusion.2
  92.0 2.8 bitcast_dynamic-update-slice_fusion.2
  94.8 158.1 %custom-call.11 = f32[16,128,128]{1,2,0:T(8,128)S(1)} custom-call(f32[16,128,128]{2,1,0:T(8,128)} %get-tuple-element.46), custom_call_target="InvertDiagBlocksLowerTriangular" | custom-call | tf_op jit(solution)/shard_map/jit(_solve_triangular)/triangular_solve | solution.py:44
  317.1 2.6 collective-permute-start.3
  321.5 10.2 %collective-permute-done.2 = f32[64,2048]{1,0:T(8,128)} collective-permute-done((f32[64,2048]{1,0:T(8,128)}, f32[64,2048]{1,0:T(8,128)}, u32[]{:S(2)}, u32[]{:S(2)}) %collective-permute-start.2) | collective-permute-done | bytes 524320 | tf_op jit(solution)/shard_map/ppermute | solution.py:23
  331.7 2.6 pad_maximum_fusion
  334.4 3.2 copy.31
  344.3 39.6 %all-reduce.3 = (f32[64]{0:T(128)S(1)}, f32[2048]{0:T(1024)S(1)}) all-reduce(f32[64]{0:T(128)S(1)} %fusion.9, f32[2048]{0:T(1024)S(1)} %dynamic-update-slice.8), channel_id=1, replica_groups=mesh['grp'=8,'mem'=4] {'grp','mem'}, use_global_device_ids=true, to_apply=%region_1.0 | all-reduce | flops 2112 | bytes 16896 | tf_op jit(solution)/shard_map/psum | solution.py:61
  387.5 40.2 %psum.51 = f32[64]{0:T(128)S(1)} all-reduce(f32[64]{0:T(128)S(1)} %get-tuple-element.439), channel_id=1, replica_groups=mesh['grp'=8,'mem'=4] {'grp','mem'}, use_global_device_ids=true, to_apply=%region_7.0 | all-reduce | flops 64 | bytes 512 | tf_op jit(solution)/shard_map/psum | solution.py:81
  430.7 3.0 scatter_custom_fusion.1
  433.7 3.6 fusion.364
  445.2 4.8 collective-permute-done.4
  450.0 5.8 collective-permute-done.5
  458.3 36.6 %all-reduce.10.cloned.1.call-done = f32[2048,64]{0,1:T(8,128)} async-done(((f32[2048,64]{0,1:T(8,128)}), f32[2048,64]{0,1:T(8,128)}) %all-reduce.10.cloned.1.call-update) | async-done | bytes 524304 | tf_op jit(solution)/shard_map/psum | solution.py:71
  564.8 2.6 collective-permute-start.7
  567.5 10.7 %collective-permute-done.6 = f32[64,2048]{1,0:T(8,128)S(1)} collective-permute-done((f32[64,2048]{1,0:T(8,128)S(1)}, f32[64,2048]{1,0:T(8,128)S(1)}, u32[]{:S(2)}, u32[]{:S(2)}) %collective-permute-start.6) | collective-permute-done | bytes 524320 | tf_op jit(solution)/shard_map/ppermute | solution.py:23
  579.4 3.2 copy.35
  589.4 40.3 %all-reduce.1 = f32[2048]{0:T(1024)S(1)} all-reduce(f32[2048]{0:T(1024)S(1)} %dynamic-update-slice.9), channel_id=3, replica_groups=mesh['grp'=8,'mem'=4] {'grp','mem'}, use_global_device_ids=true, to_apply=%add.1 | all-reduce | flops 2048 | bytes 16384
  633.3 39.7 %psum.53 = f32[64]{0:T(128)S(1)} all-reduce(f32[64]{0:T(128)S(1)} %get-tuple-element.481), channel_id=1, replica_groups=mesh['grp'=8,'mem'=4] {'grp','mem'}, use_global_device_ids=true, to_apply=%region_13.0 | all-reduce | flops 64 | bytes 512 | tf_op jit(solution)/shard_map/psum | solution.py:81
  675.9 3.0 scatter_custom_fusion.2
  678.9 3.6 fusion.363
  690.6 4.5 collective-permute-done.8
  695.1 5.3 collective-permute-done.9
  702.7 37.4 %all-reduce.12.cloned.1.call-done = f32[2048,64]{0,1:T(8,128)} async-done(((f32[2048,64]{0,1:T(8,128)}), f32[2048,64]{0,1:T(8,128)}) %all-reduce.12.cloned.1.call-update) | async-done | bytes 524304 | tf_op jit(solution)/shard_map/psum | solution.py:71
  809.7 2.6 collective-permute-start.11
  812.4 10.7 %collective-permute-done.10 = f32[64,2048]{1,0:T(8,128)S(1)} collective-permute-done((f32[64,2048]{1,0:T(8,128)S(1)}, f32[64,2048]{1,0:T(8,128)S(1)}, u32[]{:S(2)}, u32[]{:S(2)}) %collective-permute-start.10) | collective-permute-done | bytes 524320 | tf_op jit(solution)/shard_map/ppermute | solution.py:23
  824.3 3.2 copy.39
  833.5 40.3 %all-reduce.2 = f32[2048]{0:T(1024)S(1)} all-reduce(f32[2048]{0:T(1024)S(1)} %dynamic-update-slice.10), channel_id=4, replica_groups=mesh['grp'=8,'mem'=4] {'grp','mem'}, use_global_device_ids=true, to_apply=%add.2 | all-reduce | flops 2048 | bytes 16384
  875.7 39.7 %psum.55 = f32[64]{0:T(128)S(1)} all-reduce(f32[64]{0:T(128)S(1)} %get-tuple-element.523), channel_id=1, replica_groups=mesh['grp'=8,'mem'=4] {'grp','mem'}, use_global_device_ids=true, to_apply=%region_19.0 | all-reduce | flops 64 | bytes 512 | tf_op jit(solution)/shard_map/psum | solution.py:81
  (662 shorter events, 282.1 us)
Async XLA Ops:
  7.2 1.2 copy-start
  7.2 245.8 %all-reduce.8.cloned.1.call-start = ((), (), s32[]{:S(2)}) async-start(), calls=%async_computation | async-start | bytes 1048576 | tf_op jit(solution)/shard_map/psum | solution.py:71
  19.5 16.1 %collective-permute-start = (f32[64,2048]{1,0:T(8,128)}, f32[64,2048]{1,0:T(8,128)}, u32[]{:S(2)}, u32[]{:S(2)}) collective-permute-start(f32[64,2048]{1,0:T(8,128)} %copy.29), channel_id=1, source_target_pairs={{4,0},{8,4},{12,8},{16,12},{20,16},{24,20},{28,24},{0,28},{5,1},{9... | collective-permute-start | bytes 1572872 | tf_op jit(solution)/shard_map/ppermute | solution.py:13
  24.0 12.4 %collective-permute-start.1 = (f32[64,2048]{1,0:T(8,128)}, f32[64,2048]{1,0:T(8,128)S(1)}, u32[]{:S(2)}, u32[]{:S(2)}) collective-permute-start(f32[64,2048]{1,0:T(8,128)} %copy.30), channel_id=1, source_target_pairs={{28,0},{0,4},{4,8},{8,12},{12,16},{16,20},{20,24},{24,28},{29,1},{... | collective-permute-start | bytes 1572872 | tf_op jit(solution)/shard_map/ppermute | solution.py:13
  38.4 456.5 %all-reduce.10.cloned.1.call-start = ((), (), s32[]{:S(2)}) async-start(), calls=%async_computation.1 | async-start | bytes 1048576 | tf_op jit(solution)/shard_map/psum | solution.py:71
  253.0 39.3 %copy-start.1 = (f32[2048,2048]{1,0:T(8,128)S(1)}, f32[2048,2048]{1,0:T(8,128)}, u32[]{:S(2)}) copy-start(f32[2048,2048]{1,0:T(8,128)} %get-tuple-element.572) | copy-start | bytes 50331652
  273.3 46.5 %copy-start.2 = (bf16[8,256,256]{2,1,0:T(8,128)(2,1)S(1)}, bf16[8,256,256]{2,1,0:T(8,128)(2,1)}, u32[]{:S(2)}) copy-start(bf16[8,256,256]{2,1,0:T(8,128)(2,1)} %param.14) | copy-start | bytes 3145732
  293.5 46.7 %copy-start.7 = (bf16[8,24,256]{2,1,0:T(8,128)(2,1)S(1)}, bf16[8,24,256]{2,1,0:T(8,128)(2,1)}, u32[]{:S(2)}) copy-start(bf16[8,24,256]{2,1,0:T(8,128)(2,1)} %param.15) | copy-start | bytes 294916
  317.1 14.6 %collective-permute-start.2 = (f32[64,2048]{1,0:T(8,128)}, f32[64,2048]{1,0:T(8,128)}, u32[]{:S(2)}, u32[]{:S(2)}) collective-permute-start(f32[64,2048]{1,0:T(8,128)} %bitcast.39), channel_id=1, source_target_pairs={{0,4},{4,8},{8,12},{12,16},{16,20},{20,24},{24,28},{28,0},{1,5},{5... | collective-permute-start | bytes 1572872 | tf_op jit(solution)/shard_map/ppermute | solution.py:23
  317.1 14.6 %collective-permute-start.3 = (f32[64,2048]{1,0:T(8,128)}, f32[64,2048]{1,0:T(8,128)}, u32[]{:S(2)}, u32[]{:S(2)}) collective-permute-start(f32[64,2048]{1,0:T(8,128)} %bitcast.39), channel_id=1, source_target_pairs={{4,0},{8,4},{12,8},{16,12},{20,16},{24,20},{28,24},{0,28},{5,1},{9... | collective-permute-start | bytes 1572872 | tf_op jit(solution)/shard_map/ppermute | solution.py:25
  385.4 0.8 copy-start.6
  429.1 0.8 copy-start.4
  439.6 10.4 %collective-permute-start.4 = (f32[64,2048]{1,0:T(8,128)}, f32[64,2048]{1,0:T(8,128)}, u32[]{:S(2)}, u32[]{:S(2)}) collective-permute-start(f32[64,2048]{1,0:T(8,128)} %copy.33), channel_id=1, source_target_pairs={{4,0},{8,4},{12,8},{16,12},{20,16},{24,20},{28,24},{0,28},{5,1},{9... | collective-permute-start | bytes 1572872 | tf_op jit(solution)/shard_map/ppermute | solution.py:13
  442.9 12.9 %collective-permute-start.5 = (f32[64,2048]{1,0:T(8,128)}, f32[64,2048]{1,0:T(8,128)}, u32[]{:S(2)}, u32[]{:S(2)}) collective-permute-start(f32[64,2048]{1,0:T(8,128)} %copy.34), channel_id=1, source_target_pairs={{28,0},{0,4},{4,8},{8,12},{12,16},{16,20},{20,24},{24,28},{29,1},{... | collective-permute-start | bytes 1572872 | tf_op jit(solution)/shard_map/ppermute | solution.py:13
  458.1 282.0 %all-reduce.12.cloned.1.call-start = ((), (), s32[]{:S(2)}) async-start(), calls=%async_computation.2 | async-start | bytes 1048576 | tf_op jit(solution)/shard_map/psum | solution.py:71
  564.8 13.4 %collective-permute-start.6 = (f32[64,2048]{1,0:T(8,128)S(1)}, f32[64,2048]{1,0:T(8,128)S(1)}, u32[]{:S(2)}, u32[]{:S(2)}) collective-permute-start(f32[64,2048]{1,0:T(8,128)S(1)} %bitcast.583), channel_id=1, source_target_pairs={{0,4},{4,8},{8,12},{12,16},{16,20},{20,24},{24,28},{28,0},{1,5},{5... | collective-permute-start | bytes 1572872 | tf_op jit(solution)/shard_map/ppermute | solution.py:23
  564.8 13.3 %collective-permute-start.7 = (f32[64,2048]{1,0:T(8,128)S(1)}, f32[64,2048]{1,0:T(8,128)S(1)}, u32[]{:S(2)}, u32[]{:S(2)}) collective-permute-start(f32[64,2048]{1,0:T(8,128)S(1)} %bitcast.584), channel_id=1, source_target_pairs={{4,0},{8,4},{12,8},{16,12},{20,16},{24,20},{28,24},{0,28},{5,1},{9... | collective-permute-start | bytes 1572872 | tf_op jit(solution)/shard_map/ppermute | solution.py:25
  631.2 0.8 copy-start.5
  674.3 0.8 copy-start.3
  684.9 10.2 %collective-permute-start.8 = (f32[64,2048]{1,0:T(8,128)}, f32[64,2048]{1,0:T(8,128)}, u32[]{:S(2)}, u32[]{:S(2)}) collective-permute-start(f32[64,2048]{1,0:T(8,128)} %copy.37), channel_id=1, source_target_pairs={{4,0},{8,4},{12,8},{16,12},{20,16},{24,20},{28,24},{0,28},{5,1},{9... | collective-permute-start | bytes 1572872 | tf_op jit(solution)/shard_map/ppermute | solution.py:13
  688.1 12.3 %collective-permute-start.9 = (f32[64,2048]{1,0:T(8,128)}, f32[64,2048]{1,0:T(8,128)}, u32[]{:S(2)}, u32[]{:S(2)}) collective-permute-start(f32[64,2048]{1,0:T(8,128)} %copy.38), channel_id=1, source_target_pairs={{28,0},{0,4},{4,8},{8,12},{12,16},{16,20},{20,24},{24,28},{29,1},{... | collective-permute-start | bytes 1572872 | tf_op jit(solution)/shard_map/ppermute | solution.py:13
  809.7 13.4 %collective-permute-start.10 = (f32[64,2048]{1,0:T(8,128)S(1)}, f32[64,2048]{1,0:T(8,128)S(1)}, u32[]{:S(2)}, u32[]{:S(2)}) collective-permute-start(f32[64,2048]{1,0:T(8,128)S(1)} %bitcast.580), channel_id=1, source_target_pairs={{0,4},{4,8},{8,12},{12,16},{16,20},{20,24},{24,28},{28,0},{1,5},{5... | collective-permute-start | bytes 1572872 | tf_op jit(solution)/shard_map/ppermute | solution.py:23
  809.7 13.3 %collective-permute-start.11 = (f32[64,2048]{1,0:T(8,128)S(1)}, f32[64,2048]{1,0:T(8,128)S(1)}, u32[]{:S(2)}, u32[]{:S(2)}) collective-permute-start(f32[64,2048]{1,0:T(8,128)S(1)} %bitcast.581), channel_id=1, source_target_pairs={{4,0},{8,4},{12,8},{16,12},{20,16},{24,20},{28,24},{0,28},{5,1},{9... | collective-permute-start | bytes 1572872 | tf_op jit(solution)/shard_map/ppermute | solution.py:25
  875.1 42.8 %copy-start.8 = (f32[8,64,256]{2,1,0:T(8,128)}, f32[8,64,256]{2,1,0:T(8,128)S(1)}, u32[]{:S(2)}) copy-start(f32[8,64,256]{2,1,0:T(8,128)S(1)} %multiply_subtract_fusion) | copy-start | bytes 1572868
Sparse Core Ops, SparseCore 0:
  38.5 39.3 all-reduce.7
  458.2 36.6 all-reduce.9
  702.8 37.2 all-reduce.11
